TPU v7x, 64 devices: a 2x2x8 block of a 4x4x8 slice. The times are simulated.
64 devices in a mesh: dp: 8 (over x, y, core), tp: 8 (over z).
Axes of the slice: x: 2, y: 2, z: 8, core: 2. Of those that a mesh axis runs over, the one named last changes fastest.
The devices are a block of a 4x4x8 slice.
Arguments:
- x: bfloat16 [16384, 4096], P(('dp', 'tp')), parts along dimension 0
- w_gate: bfloat16 [4096, 14336], P(None, 'tp')
- w_up: bfloat16 [4096, 14336], P(None, 'tp')
- w_down: bfloat16 [14336, 4096], P('tp')
Outputs:
- output: bfloat16 [16384, 4096], P(('dp', 'tp')), parts along dimension 0
There are 8 independent parts. A program takes and returns all parts, laid end to end along the dimension named above; an argument that names none is the same for every part.
All inputs are finite; a program needn't handle non-finite values.
Results may differ from a plain program's by a relative error of at most 0.016.
Values are sent between devices in bfloat16 or wider.
A program may use at most 768 MiB of HBM per device.

v0:
```python
import jax
import jax.numpy as jnp
from jax import lax
from jax.sharding import PartitionSpec as P


def solution(mesh):
    def step(x, w_gate, w_up, w_down):
        rows = lax.all_gather(x, "tp", axis=0, tiled=True)
        gate = jnp.dot(rows, w_gate, preferred_element_type=jnp.float32)
        up = jnp.dot(rows, w_up, preferred_element_type=jnp.float32)
        hidden = (jax.nn.silu(gate) * up).astype(jnp.bfloat16)
        term = jnp.dot(hidden, w_down, preferred_element_type=jnp.float32).astype(jnp.bfloat16)
        return lax.psum_scatter(term, "tp", scatter_dimension=0, tiled=True)

    return jax.shard_map(
        step,
        mesh=mesh,
        in_specs=(P(("dp", "tp"), None), P(None, "tp"), P(None, "tp"), P("tp", None)),
        out_specs=P(("dp", "tp"), None),
        check_vma=False,
    )
```

profile of v0, /device:TPU:21, one launch (start us, length us, event | category | flops | bytes accessed | tf_op | source)
XLA Modules:
  0.0 472.2 jit_solution(7669298017210004371)
XLA Ops:
  6.5 0.0 all-gather.2.cloned.1.call-start
  6.6 0.7 all-gather.2.cloned.1.call-update
  7.3 0.1 reduce-scatter.2.cloned.1.call-start
  7.4 175.3 %all-gather.2.cloned.1.call-done = bf16[2048,4096]{1,0:T(8,128)(2,1)} async-done(((bf16[256,4096]{1,0:T(8,128)(2,1)}), bf16[2048,4096]{1,0:T(8,128)(2,1)}) %all-gather.2.cloned.1.call-update) | async-done | bytes 16777232 | tf_op jit(solution)/shard_map/all_gather | solution.py:9
  182.7 39.3 %fusion = f32[2048,1792]{1,0:T(8,128)} fusion(bf16[2048,4096]{1,0:T(8,128)(2,1)} %all-gather.2.cloned.1.call-done, bf16[4096,1792]{1,0:T(8,128)(2,1)} %param.5), kind=kOutput, calls=%fused_computation.2 | convolution fusion | flops 30064771072 | bytes 46137344 | tf_op jit(solution)/shard_map/dot_general | solution.py:10
  222.0 38.9 %multiply_convert_fusion = bf16[2048,1792]{1,0:T(8,128)(2,1)S(1)} fusion(f32[2048,1792]{1,0:T(8,128)} %fusion, bf16[2048,4096]{1,0:T(8,128)(2,1)} %all-gather.2.cloned.1.call-done, bf16[4096,1792]{1,0:T(8,128)(2,1)} %param.6), kind=kOutput, calls=%fused_computation.1 | convolution fusion | flops 30086791168 | bytes 53477376 | tf_op jit(solution)/shard_map/dot_general | solution.py:11
  260.9 35.4 %convolution_convert_fusion = bf16[2048,4096]{1,0:T(8,128)(2,1)} fusion(bf16[2048,1792]{1,0:T(8,128)(2,1)S(1)} %multiply_convert_fusion, bf16[1792,4096]{1,0:T(8,128)(2,1)} %param.7), kind=kOutput, calls=%fused_computation | convolution fusion | flops 30073159680 | bytes 38797312 | tf_op jit(solution)/shard_map/dot_general | solution.py:13
  296.3 0.1 reduce-scatter.2.cloned.1.call-update
  296.4 169.0 %reduce-scatter.2.cloned.1.call-done = bf16[256,4096]{1,0:T(8,128)(2,1)} async-done(((bf16[2048,4096]{1,0:T(8,128)(2,1)}), bf16[256,4096]{1,0:T(8,128)(2,1)}) %reduce-scatter.2.cloned.1.call-update) | async-done | bytes 2097168 | tf_op jit(solution)/shard_map/reduce_scatter | solution.py:14
Async XLA Ops:
  6.5 176.1 %all-gather.2.cloned.1.call-start = ((), (), s32[]{:S(2)}) async-start(), calls=%async_computation.1 | async-start | bytes 18874368 | tf_op jit(solution)/shard_map/all_gather | solution.py:9
  7.3 458.1 %reduce-scatter.2.cloned.1.call-start = ((), (), s32[]{:S(2)}) async-start(), calls=%async_computation.2 | async-start | bytes 18874368 | tf_op jit(solution)/shard_map/reduce_scatter | solution.py:14
Sparse Core Ops, SparseCore 0:
  8.9 173.7 all-gather.1
  296.5 168.8 reduce-scatter.1
where the time goes:
time: 472 us
  waiting for transfers between devices  345 us (73%)
  matrix products  114 us (24%)
  between operations  13.4 us (3%)
    all_gather x1, waiting for transfers between devices, step(): rows = lax.all_gather(x, 'tp', axis=0, tiled=True)  175 us
    reduce_scatter x1, waiting for transfers between devices, step(): return lax.psum_scatter(term, 'tp', scatter_dimension=0, tiled=True)  169 us
    dot_general x1, matrix products, step(): gate = jnp.dot(rows, w_gate, preferred_element_type=jnp.float32)  39.3 us
    dot_general x1, matrix products, step(): up = jnp.dot(rows, w_up, preferred_element_type=jnp.float32)  38.9 us
    dot_general x1, matrix products, step(): jnp.dot(hidden, w_down, preferred_element_type=jnp.float32)  35.4 us
  transfers between devices with their start and end apart: 2, of which 2 were waited for; matrix products, arithmetic and copies ran while one was open for 0% of the time, Pallas kernels for 0%

commit v1 on v0

v1 whole, which is shorter than its diff:
```python
import functools

import jax
import jax.numpy as jnp
from jax import lax
from jax.experimental import pallas as pl
from jax.experimental.pallas import tpu as pltpu
from jax.sharding import PartitionSpec as P

MESH = pl.DeviceIdType.MESH
SUBS = 2


def _kernel(
    n,
    x_ref,
    wg_ref,
    wu_ref,
    wd_ref,
    y_ref,
    xg_ref,
    rs_ref,
    wg,
    wu,
    wd,
    hid,
    xbuf,
    sbuf,
    acc,
    ag_send,
    ag_recv,
    rs_send,
    rs_recv,
    w_sem,
    x_sem,
    y_sem,
):
    rows, _ = x_ref.shape
    hidden = wg.shape[1]
    cols = wd.shape[1]
    half = rows // 2
    piece = half // SUBS
    pair = 2 * piece
    batches = n - 1
    nt_h = 256
    nt_y = 512
    me = lax.axis_index("tp")
    right, left = lax.rem(me + 1, n), lax.rem(me + n - 1, n)

    weights = [
        pltpu.make_async_copy(src, dst, w_sem.at[i])
        for i, (src, dst) in enumerate(((wg_ref, wg), (wu_ref, wu), (wd_ref, wd)))
    ]
    own = pltpu.make_async_copy(x_ref, xbuf, x_sem.at[0])

    barrier = pltpu.get_barrier_semaphore()
    for neighbour in (left, right):
        pl.semaphore_signal(barrier, inc=1, device_id={"tp": neighbour}, device_id_type=MESH)
    pl.semaphore_wait(barrier, 2)

    def at(s, d):
        return pl.ds(s * pair + d * piece, piece)

    def gather(b, s, d, src):
        return pltpu.make_async_remote_copy(
            src_ref=src,
            dst_ref=xg_ref.at[b, at(s, d)],
            send_sem=ag_send.at[b, s, d],
            recv_sem=ag_recv.at[b, s, d],
            device_id={"tp": right if d == 0 else left},
            device_id_type=MESH,
        )

    def gather_own(b, s, d):
        start = (b if d == 0 else 1 - b) * half + s * piece
        return gather(b, s, d, x_ref.at[pl.ds(start, piece)])

    def gather_on(b, s, d):
        return gather(b + 2, s, d, xg_ref.at[b, at(s, d)])

    def reduce(b, s, d, slot):
        return pltpu.make_async_remote_copy(
            src_ref=sbuf.at[slot, pl.ds(d * piece, piece)],
            dst_ref=rs_ref.at[b, at(s, d)],
            send_sem=rs_send.at[b, s, d],
            recv_sem=rs_recv.at[b, s, d],
            device_id={"tp": left if d == 0 else right},
            device_id_type=MESH,
        )

    for b in range(2):
        for s in range(SUBS):
            for d in range(2):
                gather_own(b, s, d).start()
    own.start()
    for w in weights:
        w.start()

    def mlp_in(b):
        def step(i, carry):
            c = pl.ds(pl.multiple_of(i * nt_h, nt_h), nt_h)
            x = xbuf[...]
            gate = jnp.dot(x, wg[:, c], preferred_element_type=jnp.float32)
            up = jnp.dot(x, wu[:, c], preferred_element_type=jnp.float32)
            hid[b, :, c] = (jax.nn.silu(gate) * up).astype(jnp.bfloat16)
            return carry

        lax.fori_loop(0, hidden // nt_h, step, 0)

    own.wait()
    weights[0].wait()
    weights[1].wait()
    mlp_in(batches)

    def batch_in(b, forward):
        for s in range(SUBS):
            for d in range(2):
                gather(b, s, d, xg_ref.at[b, at(s, d)]).wait_recv()
                if forward:
                    gather_on(b, s, d).start()
            r = pl.ds(s * pair, pair)
            pltpu.make_async_copy(xg_ref.at[b, r], xbuf.at[r], x_sem.at[s]).start()
        for s in range(SUBS):
            r = pl.ds(s * pair, pair)
            pltpu.make_async_copy(xg_ref.at[b, r], xbuf.at[r], x_sem.at[s]).wait()
        mlp_in(b)

    def batch_out(b, s, slot, add):
        h = pl.ds(s * pair, pair)
        buf = pl.ds(s * pair, pair)
        if add:
            for d in range(2):
                reduce(b + 2, s, d, slot).wait_recv()
            got = pltpu.make_async_copy(rs_ref.at[b + 2, h], xbuf.at[buf], x_sem.at[s])
            got.start()
            got.wait()

        def step(i, carry):
            c = pl.ds(pl.multiple_of(i * nt_y, nt_y), nt_y)
            term = jnp.dot(hid[b, h, :], wd[:, c], preferred_element_type=jnp.float32)
            if add:
                term = term + xbuf[buf, c].astype(jnp.float32)
            sbuf[slot, :, c] = term.astype(jnp.bfloat16)
            return carry

        lax.fori_loop(0, cols // nt_y, step, 0)
        for d in range(2):
            reduce(b, s, d, slot).start()

    def in_only(b, carry):
        batch_in(b, True)
        return carry

    lax.fori_loop(0, batches - 2, in_only, 0)

    weights[2].wait()

    def in_out(i, carry):
        b = batches - 2 + i
        batch_in(b, False)
        for s in range(SUBS):
            batch_out(b, s, i * SUBS + s, False)
        return carry

    lax.fori_loop(0, 2, in_out, 0)

    def out_only(k, carry):
        i = lax.rem(k, 2)
        b = batches - 4 - 2 * (k // 2) + i
        for s in range(SUBS):
            slot = i * SUBS + s
            for d in range(2):
                reduce(b + 2, s, d, slot).wait_send()
            batch_out(b, s, slot, True)
        return carry

    lax.fori_loop(0, batches - 3, out_only, 0)

    def own_term(i, carry):
        c = pl.ds(pl.multiple_of(i * nt_y, nt_y), nt_y)
        acc[:, c] = jnp.dot(hid[batches], wd[:, c], preferred_element_type=jnp.float32)
        return carry

    lax.fori_loop(0, cols // nt_y, own_term, 0)

    for s in range(SUBS):
        for d in range(2):
            reduce(1, s, d, s).wait_send()
        batch_out(0, s, s, True)

    for t in (1, 0):
        for s in range(SUBS):
            for d in range(2):
                reduce(t, s, d, s).wait_recv()
            r = pl.ds(s * pair, pair)
            got = pltpu.make_async_copy(rs_ref.at[t, r], xbuf.at[r], x_sem.at[s])
            got.start()
            got.wait()
            for d in range(2):
                o = pl.ds((t if d == 0 else 1 - t) * half + s * piece, piece)
                total = acc[o, :] + xbuf[at(s, d), :].astype(jnp.float32)
                if t == 1:
                    acc[o, :] = total
                else:
                    slot = SUBS + s
                    if s == 0 and d == 0:
                        for e in range(2 * SUBS):
                            reduce(2, e // 2, e % 2, SUBS + e // 2).wait_send()
                    sbuf[slot, pl.ds(d * piece, piece), :] = total.astype(jnp.bfloat16)
                    pltpu.make_async_copy(
                        sbuf.at[slot, pl.ds(d * piece, piece)], y_ref.at[o], y_sem.at[s, d]
                    ).start()

    for s in range(SUBS):
        for d in range(2):
            for b in range(batches):
                gather(b, s, d, xg_ref.at[b, at(s, d)]).wait_send()
            reduce(0, s, d, s).wait_send()
            o = pl.ds((0 if d == 0 else 1) * half + s * piece, piece)
            pltpu.make_async_copy(
                sbuf.at[SUBS + s, pl.ds(d * piece, piece)], y_ref.at[o], y_sem.at[s, d]
            ).wait()


def solution(mesh):
    n = mesh.shape["tp"]

    def step(x, w_gate, w_up, w_down):
        rows, dim = x.shape
        hidden = w_gate.shape[1]
        batches = n - 1
        piece = rows // (2 * SUBS)
        flops = 6 * n * rows * dim * hidden
        wire = 2 * batches * rows * dim * 2
        any_space = pl.BlockSpec(memory_space=pltpu.MemorySpace.HBM)
        y, _, _ = pl.pallas_call(
            functools.partial(_kernel, n),
            out_shape=(
                jax.ShapeDtypeStruct((rows, dim), jnp.bfloat16),
                jax.ShapeDtypeStruct((batches, rows, dim), jnp.bfloat16),
                jax.ShapeDtypeStruct((batches, rows, dim), jnp.bfloat16),
            ),
            in_specs=[any_space] * 4,
            out_specs=(any_space,) * 3,
            scratch_shapes=[
                pltpu.VMEM(w_gate.shape, jnp.bfloat16),
                pltpu.VMEM(w_up.shape, jnp.bfloat16),
                pltpu.VMEM(w_down.shape, jnp.bfloat16),
                pltpu.VMEM((n, rows, hidden), jnp.bfloat16),
                pltpu.VMEM((rows, dim), jnp.bfloat16),
                pltpu.VMEM((2 * SUBS, 2 * piece, dim), jnp.bfloat16),
                pltpu.VMEM((rows, dim), jnp.float32),
                pltpu.SemaphoreType.DMA((batches, SUBS, 2)),
                pltpu.SemaphoreType.DMA((batches, SUBS, 2)),
                pltpu.SemaphoreType.DMA((batches, SUBS, 2)),
                pltpu.SemaphoreType.DMA((batches, SUBS, 2)),
                pltpu.SemaphoreType.DMA((3,)),
                pltpu.SemaphoreType.DMA((SUBS,)),
                pltpu.SemaphoreType.DMA((SUBS, 2)),
            ],
            compiler_params=pltpu.CompilerParams(
                collective_id=0, has_side_effects=True, vmem_limit_bytes=67043328
            ),
            cost_estimate=pl.CostEstimate(
                flops=flops, bytes_accessed=3 * w_gate.size * 2 + 4 * wire, transcendentals=n * rows * hidden
            ),
            name="mlp_ring",
        )(x, w_gate, w_up, w_down)
        return y

    return jax.shard_map(
        step,
        mesh=mesh,
        in_specs=(P(("dp", "tp"), None), P(None, "tp"), P(None, "tp"), P("tp", None)),
        out_specs=P(("dp", "tp"), None),
        check_vma=False,
    )
```

time: 472 us -> 331 us (0.70)
  waiting for transfers between devices: 345 us -> 0 us
  Pallas kernels: 0 us -> 327 us
  matrix products: 114 us -> 0 us
  between operations: 13.4 us -> 0.01 us
    pallas_call x0 -> x1, Pallas kernels: none -> 327 us  [step(): pl.pallas_call(functools.partial(_kernel, n), out_shape=(jax.ShapeDtypeSt...]
    all_gather x1 -> x0, waiting for transfers between devices: 175 us -> none  [step(): rows = lax.all_gather(x, 'tp', axis=0, tiled=True)]
    reduce_scatter x1 -> x0, waiting for transfers between devices: 169 us -> none  [step(): return lax.psum_scatter(term, 'tp', scatter_dimension=0, tiled=True)]
    dot_general x3 -> x0, matrix products: 114 us -> none  [the longest x1 39.3 us: step(): gate = jnp.dot(rows, w_gate, preferred_element_type=jnp.float32)]
  transfers between devices with their start and end apart: 2 -> 0, of which waited for: 2 -> 0; matrix products, arithmetic and copies ran while one was open for 0% -> 0% of each run, Pallas kernels for 0% -> 0%
where the time goes in v1:
time: 331 us; the launch traced here: 330 us
  Pallas kernels  327 us (99%)
    pallas_call x1, Pallas kernels, step(): pl.pallas_call(functools.partial(_kernel, n), out_shape=(jax.ShapeDtypeSt...  327 us

profile of v1, /device:TPU:21, one launch (start us, length us, event | category | flops | bytes accessed | tf_op | source)
XLA Modules:
  0.0 329.9 jit_solution(17306481772369485175)
XLA Ops:
  0.0 326.8 %mlp_ring.1 = (bf16[256,4096]{1,0:T(8,128)(2,1)}, bf16[7,256,4096]{2,1,0:T(8,128)(2,1)}, bf16[7,256,4096]{2,1,0:T(8,128)(2,1)}) custom-call(bf16[256,4096]{1,0:T(8,128)(2,1)} %x_ref.1, bf16[4096,1792]{1,0:T(8,128)(2,1)} %wg_ref.1, bf16[4096,1792]{1,0:T(8,128)(2,1)} %wu_ref.1, bf16[1792,4096]{1,0:T(8,128)(2,1)} %wd_ref.1), custom_call_target="tpu_custom_call" | custom-call | flops 90194313216 | bytes 161480704 | tf_op jit(solution)/shard_map/mlp_ring/pallas_call | solution.py:236
  326.8 3.1 copy.6

commit v2 on v1

--- a/solution.py
+++ b/solution.py
@@ -8,6 +8,7 @@
 from jax.sharding import PartitionSpec as P
 
 MESH = pl.DeviceIdType.MESH
+VMEM_LIMIT = 60 * 2**20
 SUBS = 2
 
 
@@ -33,7 +34,6 @@
     rs_recv,
     w_sem,
     x_sem,
-    y_sem,
 ):
     rows, _ = x_ref.shape
     hidden = wg.shape[1]
@@ -78,10 +78,13 @@
     def gather_on(b, s, d):
         return gather(b + 2, s, d, xg_ref.at[b, at(s, d)])
 
-    def reduce(b, s, d, slot):
+    def home(t, s, d):
+        return pl.ds((t if d == 0 else 1 - t) * half + s * piece, piece)
+
+    def reduce(b, s, d, slot, last=False):
         return pltpu.make_async_remote_copy(
             src_ref=sbuf.at[slot, pl.ds(d * piece, piece)],
-            dst_ref=rs_ref.at[b, at(s, d)],
+            dst_ref=y_ref.at[home(0, s, d)] if last else rs_ref.at[b - 1, at(s, d)],
             send_sem=rs_send.at[b, s, d],
             recv_sem=rs_recv.at[b, s, d],
             device_id={"tp": left if d == 0 else right},
@@ -110,7 +113,15 @@
     own.wait()
     weights[0].wait()
     weights[1].wait()
-    mlp_in(batches)
+    mlp_in(0)
+    weights[2].wait()
+
+    def own_term(i, carry):
+        c = pl.ds(pl.multiple_of(i * nt_y, nt_y), nt_y)
+        acc[:, c] = jnp.dot(hid[0], wd[:, c], preferred_element_type=jnp.float32)
+        return carry
+
+    lax.fori_loop(0, cols // nt_y, own_term, 0)
 
     def batch_in(b, forward):
         for s in range(SUBS):
@@ -125,13 +136,13 @@
             pltpu.make_async_copy(xg_ref.at[b, r], xbuf.at[r], x_sem.at[s]).wait()
         mlp_in(b)
 
-    def batch_out(b, s, slot, add):
+    def batch_out(b, s, slot, add, last=False):
         h = pl.ds(s * pair, pair)
         buf = pl.ds(s * pair, pair)
         if add:
             for d in range(2):
                 reduce(b + 2, s, d, slot).wait_recv()
-            got = pltpu.make_async_copy(rs_ref.at[b + 2, h], xbuf.at[buf], x_sem.at[s])
+            got = pltpu.make_async_copy(rs_ref.at[b + 1, h], xbuf.at[buf], x_sem.at[s])
             got.start()
             got.wait()
 
@@ -145,15 +156,13 @@
 
         lax.fori_loop(0, cols // nt_y, step, 0)
         for d in range(2):
-            reduce(b, s, d, slot).start()
+            reduce(b, s, d, slot, last).start()
 
     def in_only(b, carry):
         batch_in(b, True)
         return carry
 
     lax.fori_loop(0, batches - 2, in_only, 0)
-
-    weights[2].wait()
 
     def in_out(i, carry):
         b = batches - 2 + i
@@ -176,50 +185,38 @@
 
     lax.fori_loop(0, batches - 3, out_only, 0)
 
-    def own_term(i, carry):
-        c = pl.ds(pl.multiple_of(i * nt_y, nt_y), nt_y)
-        acc[:, c] = jnp.dot(hid[batches], wd[:, c], preferred_element_type=jnp.float32)
-        return carry
-
-    lax.fori_loop(0, cols // nt_y, own_term, 0)
-
     for s in range(SUBS):
         for d in range(2):
             reduce(1, s, d, s).wait_send()
-        batch_out(0, s, s, True)
-
-    for t in (1, 0):
-        for s in range(SUBS):
-            for d in range(2):
-                reduce(t, s, d, s).wait_recv()
-            r = pl.ds(s * pair, pair)
-            got = pltpu.make_async_copy(rs_ref.at[t, r], xbuf.at[r], x_sem.at[s])
-            got.start()
-            got.wait()
-            for d in range(2):
-                o = pl.ds((t if d == 0 else 1 - t) * half + s * piece, piece)
-                total = acc[o, :] + xbuf[at(s, d), :].astype(jnp.float32)
-                if t == 1:
-                    acc[o, :] = total
-                else:
-                    slot = SUBS + s
-                    if s == 0 and d == 0:
-                        for e in range(2 * SUBS):
-                            reduce(2, e // 2, e % 2, SUBS + e // 2).wait_send()
-                    sbuf[slot, pl.ds(d * piece, piece), :] = total.astype(jnp.bfloat16)
-                    pltpu.make_async_copy(
-                        sbuf.at[slot, pl.ds(d * piece, piece)], y_ref.at[o], y_sem.at[s, d]
-                    ).start()
+        batch_out(0, s, s, True, last=True)
+
+    for s in range(SUBS):
+        for d in range(2):
+            reduce(1, s, d, s).wait_recv()
+        r = pl.ds(s * pair, pair)
+        got = pltpu.make_async_copy(rs_ref.at[0, r], xbuf.at[r], x_sem.at[s])
+        got.start()
+        got.wait()
+        for d in range(2):
+            o = home(1, s, d)
+            acc[o, :] = acc[o, :] + xbuf[at(s, d), :].astype(jnp.float32)
 
     for s in range(SUBS):
         for d in range(2):
             for b in range(batches):
                 gather(b, s, d, xg_ref.at[b, at(s, d)]).wait_send()
-            reduce(0, s, d, s).wait_send()
-            o = pl.ds((0 if d == 0 else 1) * half + s * piece, piece)
-            pltpu.make_async_copy(
-                sbuf.at[SUBS + s, pl.ds(d * piece, piece)], y_ref.at[o], y_sem.at[s, d]
-            ).wait()
+            reduce(2, s, d, SUBS + s).wait_send()
+
+    for s in range(SUBS):
+        for d in range(2):
+            reduce(0, s, d, s, last=True).wait_recv()
+        for d in range(2):
+            o = home(0, s, d)
+            y_ref[o, :] = (acc[o, :] + y_ref[o, :].astype(jnp.float32)).astype(jnp.bfloat16)
+
+    for s in range(SUBS):
+        for d in range(2):
+            reduce(0, s, d, s, last=True).wait_send()
 
 
 def solution(mesh):
@@ -236,17 +233,17 @@
         y, _, _ = pl.pallas_call(
             functools.partial(_kernel, n),
             out_shape=(
-                jax.ShapeDtypeStruct((rows, dim), jnp.bfloat16),
+                pltpu.VMEM((rows, dim), jnp.bfloat16),
                 jax.ShapeDtypeStruct((batches, rows, dim), jnp.bfloat16),
-                jax.ShapeDtypeStruct((batches, rows, dim), jnp.bfloat16),
+                jax.ShapeDtypeStruct((batches - 1, rows, dim), jnp.bfloat16),
             ),
             in_specs=[any_space] * 4,
-            out_specs=(any_space,) * 3,
+            out_specs=(pl.BlockSpec(memory_space=pltpu.MemorySpace.VMEM), any_space, any_space),
             scratch_shapes=[
                 pltpu.VMEM(w_gate.shape, jnp.bfloat16),
                 pltpu.VMEM(w_up.shape, jnp.bfloat16),
                 pltpu.VMEM(w_down.shape, jnp.bfloat16),
-                pltpu.VMEM((n, rows, hidden), jnp.bfloat16),
+                pltpu.VMEM((batches, rows, hidden), jnp.bfloat16),
                 pltpu.VMEM((rows, dim), jnp.bfloat16),
                 pltpu.VMEM((2 * SUBS, 2 * piece, dim), jnp.bfloat16),
                 pltpu.VMEM((rows, dim), jnp.float32),
@@ -256,10 +253,9 @@
                 pltpu.SemaphoreType.DMA((batches, SUBS, 2)),
                 pltpu.SemaphoreType.DMA((3,)),
                 pltpu.SemaphoreType.DMA((SUBS,)),
-                pltpu.SemaphoreType.DMA((SUBS, 2)),
             ],
             compiler_params=pltpu.CompilerParams(
-                collective_id=0, has_side_effects=True, vmem_limit_bytes=67043328
+                collective_id=0, has_side_effects=True, vmem_limit_bytes=VMEM_LIMIT
             ),
             cost_estimate=pl.CostEstimate(
                 flops=flops, bytes_accessed=3 * w_gate.size * 2 + 4 * wire, transcendentals=n * rows * hidden

time: 331 us -> 327 us (0.988)
  no operation moved by 1% of the time
where the time goes in v2:
time: 327 us; the launch traced here: 326 us
  Pallas kernels  325 us (99%)
    pallas_call x1, Pallas kernels, step(): pl.pallas_call(functools.partial(_kernel, n), out_shape=(pltpu.VMEM((rows...  325 us

profile of v2, /device:TPU:21, one launch (start us, length us, event | category | flops | bytes accessed | tf_op | source)
XLA Modules:
  0.0 325.9 jit_solution(6336414434033929645)
XLA Ops:
  0.0 324.5 %mlp_ring.1 = (bf16[256,4096]{1,0:T(8,128)(2,1)S(1)}, bf16[7,256,4096]{2,1,0:T(8,128)(2,1)}, bf16[6,256,4096]{2,1,0:T(8,128)(2,1)}) custom-call(bf16[256,4096]{1,0:T(8,128)(2,1)} %x_ref.1, bf16[4096,1792]{1,0:T(8,128)(2,1)} %wg_ref.1, bf16[4096,1792]{1,0:T(8,128)(2,1)} %wu_ref.1, bf16[1792,4096]{1,0:T(8,128)(2,1)} %wd_ref.1), custom_call_target="tpu_custom_call" | custom-call | flops 90194313216 | bytes 161480704 | tf_op jit(solution)/shard_map/mlp_ring/pallas_call | solution.py:233
  324.5 1.3 copy.6

commit v3 on v2

--- a/solution.py
+++ b/solution.py
@@ -8,7 +8,7 @@
 from jax.sharding import PartitionSpec as P
 
 MESH = pl.DeviceIdType.MESH
-VMEM_LIMIT = 60 * 2**20
+VMEM_LIMIT = 61 * 2**20 + 2**19
 SUBS = 2
 
 
@@ -34,6 +34,7 @@
     rs_recv,
     w_sem,
     x_sem,
+    r_sem,
 ):
     rows, _ = x_ref.shape
     hidden = wg.shape[1]
@@ -47,11 +48,12 @@
     me = lax.axis_index("tp")
     right, left = lax.rem(me + 1, n), lax.rem(me + n - 1, n)
 
+    own = pltpu.make_async_copy(x_ref, xbuf.at[0], x_sem.at[0])
+    own.start()
     weights = [
         pltpu.make_async_copy(src, dst, w_sem.at[i])
         for i, (src, dst) in enumerate(((wg_ref, wg), (wu_ref, wu), (wd_ref, wd)))
     ]
-    own = pltpu.make_async_copy(x_ref, xbuf, x_sem.at[0])
 
     barrier = pltpu.get_barrier_semaphore()
     for neighbour in (left, right):
@@ -73,7 +75,7 @@
 
     def gather_own(b, s, d):
         start = (b if d == 0 else 1 - b) * half + s * piece
-        return gather(b, s, d, x_ref.at[pl.ds(start, piece)])
+        return gather(b, s, d, xbuf.at[0, pl.ds(start, piece)])
 
     def gather_on(b, s, d):
         return gather(b + 2, s, d, xg_ref.at[b, at(s, d)])
@@ -91,30 +93,47 @@
             device_id_type=MESH,
         )
 
+    own.wait()
     for b in range(2):
         for s in range(SUBS):
             for d in range(2):
                 gather_own(b, s, d).start()
-    own.start()
     for w in weights:
         w.start()
 
-    def mlp_in(b):
+    def mlp_in(x_slot, h_slot):
         def step(i, carry):
             c = pl.ds(pl.multiple_of(i * nt_h, nt_h), nt_h)
-            x = xbuf[...]
+            x = xbuf[x_slot]
             gate = jnp.dot(x, wg[:, c], preferred_element_type=jnp.float32)
             up = jnp.dot(x, wu[:, c], preferred_element_type=jnp.float32)
-            hid[b, :, c] = (jax.nn.silu(gate) * up).astype(jnp.bfloat16)
+            hid[h_slot, :, c] = (jax.nn.silu(gate) * up).astype(jnp.bfloat16)
             return carry
 
         lax.fori_loop(0, hidden // nt_h, step, 0)
 
-    own.wait()
-    weights[0].wait()
-    weights[1].wait()
-    mlp_in(0)
-    weights[2].wait()
+    def x_slot(b):
+        return lax.rem(b + 1, 2)
+
+    def x_load(b):
+        return pltpu.make_async_copy(xg_ref.at[b], xbuf.at[x_slot(b)], x_sem.at[x_slot(b)])
+
+    def receive(b, forward):
+        for s in range(SUBS):
+            for d in range(2):
+                gather(b, s, d, xg_ref.at[b, at(s, d)]).wait_recv()
+                if forward:
+                    gather_on(b, s, d).start()
+
+    def batch_in(b):
+        x_load(b).wait()
+        mlp_in(x_slot(b), b)
+
+    receive(0, True)
+    x_load(0).start()
+    for w in weights:
+        w.wait()
+    mlp_in(0, 0)
 
     def own_term(i, carry):
         c = pl.ds(pl.multiple_of(i * nt_y, nt_y), nt_y)
@@ -123,34 +142,42 @@
 
     lax.fori_loop(0, cols // nt_y, own_term, 0)
 
-    def batch_in(b, forward):
+    receive(1, True)
+    for b in range(2):
         for s in range(SUBS):
             for d in range(2):
-                gather(b, s, d, xg_ref.at[b, at(s, d)]).wait_recv()
-                if forward:
-                    gather_on(b, s, d).start()
-            r = pl.ds(s * pair, pair)
-            pltpu.make_async_copy(xg_ref.at[b, r], xbuf.at[r], x_sem.at[s]).start()
-        for s in range(SUBS):
-            r = pl.ds(s * pair, pair)
-            pltpu.make_async_copy(xg_ref.at[b, r], xbuf.at[r], x_sem.at[s]).wait()
-        mlp_in(b)
+                gather_own(b, s, d).wait_send()
+    x_load(1).start()
+    batch_in(0)
+
+    def in_only(b, carry):
+        receive(b, True)
+        x_load(b).start()
+        batch_in(b - 1)
+        return carry
+
+    lax.fori_loop(2, batches - 2, in_only, 0)
+    batch_in(batches - 3)
+
+    def fetch(b, s):
+        for d in range(2):
+            reduce(b + 2, s, d, 0).wait_recv()
+        load(b, s).start()
+
+    def load(b, s):
+        r = pl.ds(s * pair, pair)
+        return pltpu.make_async_copy(rs_ref.at[b + 1, r], xbuf.at[0, r], r_sem.at[s])
 
     def batch_out(b, s, slot, add, last=False):
         h = pl.ds(s * pair, pair)
-        buf = pl.ds(s * pair, pair)
         if add:
-            for d in range(2):
-                reduce(b + 2, s, d, slot).wait_recv()
-            got = pltpu.make_async_copy(rs_ref.at[b + 1, h], xbuf.at[buf], x_sem.at[s])
-            got.start()
-            got.wait()
+            load(b, s).wait()
 
         def step(i, carry):
             c = pl.ds(pl.multiple_of(i * nt_y, nt_y), nt_y)
             term = jnp.dot(hid[b, h, :], wd[:, c], preferred_element_type=jnp.float32)
             if add:
-                term = term + xbuf[buf, c].astype(jnp.float32)
+                term = term + xbuf[0, h, c].astype(jnp.float32)
             sbuf[slot, :, c] = term.astype(jnp.bfloat16)
             return carry
 
@@ -158,52 +185,61 @@
         for d in range(2):
             reduce(b, s, d, slot, last).start()
 
-    def in_only(b, carry):
-        batch_in(b, True)
-        return carry
-
-    lax.fori_loop(0, batches - 2, in_only, 0)
-
     def in_out(i, carry):
         b = batches - 2 + i
-        batch_in(b, False)
+        receive(b, False)
+        x_load(b).start()
+        batch_in(b)
         for s in range(SUBS):
             batch_out(b, s, i * SUBS + s, False)
         return carry
 
     lax.fori_loop(0, 2, in_out, 0)
 
-    def out_only(k, carry):
-        i = lax.rem(k, 2)
-        b = batches - 4 - 2 * (k // 2) + i
-        for s in range(SUBS):
-            slot = i * SUBS + s
+    def order(k):
+        return batches - 4 - 2 * (k // 2) + lax.rem(k, 2)
+
+    def out_pair(k, ahead):
+        b = order(k)
+        for s in range(SUBS):
+            if s + 1 < SUBS:
+                fetch(b, s + 1)
+            elif ahead:
+                fetch(order(k + 1), 0)
+            slot = lax.rem(k, 2) * SUBS + s
             for d in range(2):
                 reduce(b + 2, s, d, slot).wait_send()
             batch_out(b, s, slot, True)
+
+    def out_only(k, carry):
+        out_pair(k, True)
         return carry
 
-    lax.fori_loop(0, batches - 3, out_only, 0)
+    fetch(order(0), 0)
+    lax.fori_loop(0, batches - 4, out_only, 0)
+    out_pair(batches - 4, False)
+
+    for s in range(SUBS):
+        for d in range(2):
+            reduce(1, s, d, s).wait_recv()
+    mine = pltpu.make_async_copy(rs_ref.at[0], xbuf.at[1], x_sem.at[1])
+    mine.start()
 
     for s in range(SUBS):
         for d in range(2):
             reduce(1, s, d, s).wait_send()
+        fetch(0, s)
         batch_out(0, s, s, True, last=True)
 
-    for s in range(SUBS):
-        for d in range(2):
-            reduce(1, s, d, s).wait_recv()
-        r = pl.ds(s * pair, pair)
-        got = pltpu.make_async_copy(rs_ref.at[0, r], xbuf.at[r], x_sem.at[s])
-        got.start()
-        got.wait()
+    mine.wait()
+    for s in range(SUBS):
         for d in range(2):
             o = home(1, s, d)
-            acc[o, :] = acc[o, :] + xbuf[at(s, d), :].astype(jnp.float32)
-
-    for s in range(SUBS):
-        for d in range(2):
-            for b in range(batches):
+            acc[o, :] = acc[o, :] + xbuf[1, at(s, d), :].astype(jnp.float32)
+
+    for s in range(SUBS):
+        for d in range(2):
+            for b in range(2, batches):
                 gather(b, s, d, xg_ref.at[b, at(s, d)]).wait_send()
             reduce(2, s, d, SUBS + s).wait_send()
 
@@ -244,7 +280,7 @@
                 pltpu.VMEM(w_up.shape, jnp.bfloat16),
                 pltpu.VMEM(w_down.shape, jnp.bfloat16),
                 pltpu.VMEM((batches, rows, hidden), jnp.bfloat16),
-                pltpu.VMEM((rows, dim), jnp.bfloat16),
+                pltpu.VMEM((2, rows, dim), jnp.bfloat16),
                 pltpu.VMEM((2 * SUBS, 2 * piece, dim), jnp.bfloat16),
                 pltpu.VMEM((rows, dim), jnp.float32),
                 pltpu.SemaphoreType.DMA((batches, SUBS, 2)),
@@ -252,6 +288,7 @@
                 pltpu.SemaphoreType.DMA((batches, SUBS, 2)),
                 pltpu.SemaphoreType.DMA((batches, SUBS, 2)),
                 pltpu.SemaphoreType.DMA((3,)),
+                pltpu.SemaphoreType.DMA((2,)),
                 pltpu.SemaphoreType.DMA((SUBS,)),
             ],
             compiler_params=pltpu.CompilerParams(

time: 327 us -> 327 us (level)
  no operation moved by 1% of the time
where the time goes in v3:
time: 327 us
  Pallas kernels  326 us (100%)
    pallas_call x1, Pallas kernels, step(): pl.pallas_call(functools.partial(_kernel, n), out_shape=(pltpu.VMEM((rows...  326 us

profile of v3, /device:TPU:21, one launch (start us, length us, event | category | flops | bytes accessed | tf_op | source)
XLA Modules:
  0.0 327.0 jit_solution(6137230678241104324)
XLA Ops:
  0.0 325.7 %mlp_ring.1 = (bf16[256,4096]{1,0:T(8,128)(2,1)S(1)}, bf16[7,256,4096]{2,1,0:T(8,128)(2,1)}, bf16[6,256,4096]{2,1,0:T(8,128)(2,1)}) custom-call(bf16[256,4096]{1,0:T(8,128)(2,1)} %x_ref.1, bf16[4096,1792]{1,0:T(8,128)(2,1)} %wg_ref.1, bf16[4096,1792]{1,0:T(8,128)(2,1)} %wu_ref.1, bf16[1792,4096]{1,0:T(8,128)(2,1)} %wd_ref.1), custom_call_target="tpu_custom_call" | custom-call | flops 90194313216 | bytes 161480704 | tf_op jit(solution)/shard_map/mlp_ring/pallas_call | solution.py:269
  325.7 1.3 copy.6

commit v4 on v3

--- a/solution.py
+++ b/solution.py
@@ -49,7 +49,6 @@
     right, left = lax.rem(me + 1, n), lax.rem(me + n - 1, n)
 
     own = pltpu.make_async_copy(x_ref, xbuf.at[0], x_sem.at[0])
-    own.start()
     weights = [
         pltpu.make_async_copy(src, dst, w_sem.at[i])
         for i, (src, dst) in enumerate(((wg_ref, wg), (wu_ref, wu), (wd_ref, wd)))
@@ -75,7 +74,7 @@
 
     def gather_own(b, s, d):
         start = (b if d == 0 else 1 - b) * half + s * piece
-        return gather(b, s, d, xbuf.at[0, pl.ds(start, piece)])
+        return gather(b, s, d, x_ref.at[pl.ds(start, piece)])
 
     def gather_on(b, s, d):
         return gather(b + 2, s, d, xg_ref.at[b, at(s, d)])
@@ -93,11 +92,11 @@
             device_id_type=MESH,
         )
 
-    own.wait()
     for b in range(2):
         for s in range(SUBS):
             for d in range(2):
                 gather_own(b, s, d).start()
+    own.start()
     for w in weights:
         w.start()
 
@@ -131,6 +130,7 @@
 
     receive(0, True)
     x_load(0).start()
+    own.wait()
     for w in weights:
         w.wait()
     mlp_in(0, 0)
@@ -143,10 +143,6 @@
     lax.fori_loop(0, cols // nt_y, own_term, 0)
 
     receive(1, True)
-    for b in range(2):
-        for s in range(SUBS):
-            for d in range(2):
-                gather_own(b, s, d).wait_send()
     x_load(1).start()
     batch_in(0)
 
@@ -239,7 +235,7 @@
 
     for s in range(SUBS):
         for d in range(2):
-            for b in range(2, batches):
+            for b in range(batches):
                 gather(b, s, d, xg_ref.at[b, at(s, d)]).wait_send()
             reduce(2, s, d, SUBS + s).wait_send()
 

time: 327 us -> 326 us (level)
  no operation moved by 1% of the time
where the time goes in v4:
time: 326 us
  Pallas kernels  325 us (100%)
    pallas_call x1, Pallas kernels, step(): pl.pallas_call(functools.partial(_kernel, n), out_shape=(pltpu.VMEM((rows...  325 us

profile of v4, /device:TPU:21, one launch (start us, length us, event | category | flops | bytes accessed | tf_op | source)
XLA Modules:
  0.0 325.9 jit_solution(2934288096702014318)
XLA Ops:
  0.0 324.5 %mlp_ring.1 = (bf16[256,4096]{1,0:T(8,128)(2,1)S(1)}, bf16[7,256,4096]{2,1,0:T(8,128)(2,1)}, bf16[6,256,4096]{2,1,0:T(8,128)(2,1)}) custom-call(bf16[256,4096]{1,0:T(8,128)(2,1)} %x_ref.1, bf16[4096,1792]{1,0:T(8,128)(2,1)} %wg_ref.1, bf16[4096,1792]{1,0:T(8,128)(2,1)} %wu_ref.1, bf16[1792,4096]{1,0:T(8,128)(2,1)} %wd_ref.1), custom_call_target="tpu_custom_call" | custom-call | flops 90194313216 | bytes 161480704 | tf_op jit(solution)/shard_map/mlp_ring/pallas_call | solution.py:265
  324.6 1.3 copy.6

commit v5 on v4

--- a/solution.py
+++ b/solution.py
@@ -35,6 +35,7 @@
     w_sem,
     x_sem,
     r_sem,
+    ready,
 ):
     rows, _ = x_ref.shape
     hidden = wg.shape[1]
@@ -55,9 +56,9 @@
     ]
 
     barrier = pltpu.get_barrier_semaphore()
-    for neighbour in (left, right):
-        pl.semaphore_signal(barrier, inc=1, device_id={"tp": neighbour}, device_id_type=MESH)
-    pl.semaphore_wait(barrier, 2)
+    pl.semaphore_signal(barrier, inc=1, device_id={"tp": left}, device_id_type=MESH)
+    pl.semaphore_wait(barrier, 1)
+    pl.semaphore_signal(ready, inc=1, device_id={"tp": right}, device_id_type=MESH)
 
     def at(s, d):
         return pl.ds(s * pair + d * piece, piece)
@@ -92,9 +93,11 @@
             device_id_type=MESH,
         )
 
-    for b in range(2):
-        for s in range(SUBS):
-            for d in range(2):
+    for d in range(2):
+        if d == 1:
+            pl.semaphore_wait(ready, 1)
+        for b in range(2):
+            for s in range(SUBS):
                 gather_own(b, s, d).start()
     own.start()
     for w in weights:
@@ -286,6 +289,7 @@
                 pltpu.SemaphoreType.DMA((3,)),
                 pltpu.SemaphoreType.DMA((2,)),
                 pltpu.SemaphoreType.DMA((SUBS,)),
+                pltpu.SemaphoreType.REGULAR,
             ],
             compiler_params=pltpu.CompilerParams(
                 collective_id=0, has_side_effects=True, vmem_limit_bytes=VMEM_LIMIT

time: 326 us -> 326 us (level)
  no operation moved by 1% of the time
where the time goes in v5:
time: 326 us
  Pallas kernels  324 us (99%)
    pallas_call x1, Pallas kernels, step(): pl.pallas_call(functools.partial(_kernel, n), out_shape=(pltpu.VMEM((rows...  324 us

profile of v5, /device:TPU:21, one launch (start us, length us, event | category | flops | bytes accessed | tf_op | source)
XLA Modules:
  0.0 325.6 jit_solution(6091132492704526503)
XLA Ops:
  0.0 324.3 %mlp_ring.1 = (bf16[256,4096]{1,0:T(8,128)(2,1)S(1)}, bf16[7,256,4096]{2,1,0:T(8,128)(2,1)}, bf16[6,256,4096]{2,1,0:T(8,128)(2,1)}) custom-call(bf16[256,4096]{1,0:T(8,128)(2,1)} %x_ref.1, bf16[4096,1792]{1,0:T(8,128)(2,1)} %wg_ref.1, bf16[4096,1792]{1,0:T(8,128)(2,1)} %wu_ref.1, bf16[1792,4096]{1,0:T(8,128)(2,1)} %wd_ref.1), custom_call_target="tpu_custom_call" | custom-call | flops 90194313216 | bytes 161480704 | tf_op jit(solution)/shard_map/mlp_ring/pallas_call | solution.py:268
  324.3 1.3 copy.6

commit v6 on v5

--- a/solution.py
+++ b/solution.py
@@ -158,25 +158,25 @@
     lax.fori_loop(2, batches - 2, in_only, 0)
     batch_in(batches - 3)
 
-    def fetch(b, s):
+    def load(b, s, p):
+        r = pl.ds(s * pair, pair)
+        return pltpu.make_async_copy(rs_ref.at[b + 1, r], xbuf.at[0, pl.ds(p * pair, pair)], r_sem.at[p])
+
+    def fetch(b, s, p):
         for d in range(2):
             reduce(b + 2, s, d, 0).wait_recv()
-        load(b, s).start()
-
-    def load(b, s):
-        r = pl.ds(s * pair, pair)
-        return pltpu.make_async_copy(rs_ref.at[b + 1, r], xbuf.at[0, r], r_sem.at[s])
-
-    def batch_out(b, s, slot, add, last=False):
+        load(b, s, p).start()
+
+    def batch_out(b, s, slot, p=None, last=False):
         h = pl.ds(s * pair, pair)
-        if add:
-            load(b, s).wait()
+        if p is not None:
+            load(b, s, p).wait()
 
         def step(i, carry):
             c = pl.ds(pl.multiple_of(i * nt_y, nt_y), nt_y)
             term = jnp.dot(hid[b, h, :], wd[:, c], preferred_element_type=jnp.float32)
-            if add:
-                term = term + xbuf[0, h, c].astype(jnp.float32)
+            if p is not None:
+                term = term + xbuf[0, p * pair : (p + 1) * pair, c].astype(jnp.float32)
             sbuf[slot, :, c] = term.astype(jnp.bfloat16)
             return carry
 
@@ -190,46 +190,40 @@
         x_load(b).start()
         batch_in(b)
         for s in range(SUBS):
-            batch_out(b, s, i * SUBS + s, False)
+            batch_out(b, s, i * SUBS + s)
         return carry
 
     lax.fori_loop(0, 2, in_out, 0)
 
-    def order(k):
-        return batches - 4 - 2 * (k // 2) + lax.rem(k, 2)
-
-    def out_pair(k, ahead):
-        b = order(k)
-        for s in range(SUBS):
-            if s + 1 < SUBS:
-                fetch(b, s + 1)
-            elif ahead:
-                fetch(order(k + 1), 0)
-            slot = lax.rem(k, 2) * SUBS + s
-            for d in range(2):
-                reduce(b + 2, s, d, slot).wait_send()
-            batch_out(b, s, slot, True)
-
-    def out_only(k, carry):
-        out_pair(k, True)
-        return carry
-
-    fetch(order(0), 0)
-    lax.fori_loop(0, batches - 4, out_only, 0)
-    out_pair(batches - 4, False)
+    order = [(b, s) for b in (batches - 2, batches - 1) for s in range(SUBS)]
+    for r in range(n // 2 - 2, 0, -1):
+        two = (2 * r - 1, 2 * r) if r == n // 2 - 2 else (2 * r, 2 * r - 1)
+        order += [(b, s) for s in range(SUBS) for b in two]
+    order += [(0, s) for s in range(SUBS)]
+    slots = 2 * SUBS
+    mine = pltpu.make_async_copy(rs_ref.at[0], xbuf.at[1], x_sem.at[1])
+
+    def back(k):
+        b, s = order[k]
+        return k - order.index((b + 2, s))
+
+    fetched = -1
+    for k in range(slots, len(order)):
+        b, s = order[k]
+        if fetched < k:
+            fetch(b, s, k % 2)
+            fetched = k
+        if k + 1 < len(order) and back(k + 1) >= slots:
+            fetch(*order[k + 1], (k + 1) % 2)
+            fetched = k + 1
+        for d in range(2):
+            reduce(*order[k - slots], d, k % slots).wait_send()
+        batch_out(b, s, k % slots, k % 2, last=b == 0)
 
     for s in range(SUBS):
         for d in range(2):
             reduce(1, s, d, s).wait_recv()
-    mine = pltpu.make_async_copy(rs_ref.at[0], xbuf.at[1], x_sem.at[1])
     mine.start()
-
-    for s in range(SUBS):
-        for d in range(2):
-            reduce(1, s, d, s).wait_send()
-        fetch(0, s)
-        batch_out(0, s, s, True, last=True)
-
     mine.wait()
     for s in range(SUBS):
         for d in range(2):
@@ -240,7 +234,9 @@
         for d in range(2):
             for b in range(batches):
                 gather(b, s, d, xg_ref.at[b, at(s, d)]).wait_send()
-            reduce(2, s, d, SUBS + s).wait_send()
+    for k in range(len(order) - slots, len(order) - SUBS):
+        for d in range(2):
+            reduce(*order[k], d, k % slots).wait_send()
 
     for s in range(SUBS):
         for d in range(2):

time: 326 us -> 326 us (level)
  no operation moved by 1% of the time
where the time goes in v6:
time: 326 us
  Pallas kernels  324 us (99%)
    pallas_call x1, Pallas kernels, step(): pl.pallas_call(functools.partial(_kernel, n), out_shape=(pltpu.VMEM((rows...  324 us

profile of v6, /device:TPU:21, one launch (start us, length us, event | category | flops | bytes accessed | tf_op | source)
XLA Modules:
  0.0 325.6 jit_solution(7899046932037808287)
XLA Ops:
  0.0 324.3 %mlp_ring.1 = (bf16[256,4096]{1,0:T(8,128)(2,1)S(1)}, bf16[7,256,4096]{2,1,0:T(8,128)(2,1)}, bf16[6,256,4096]{2,1,0:T(8,128)(2,1)}) custom-call(bf16[256,4096]{1,0:T(8,128)(2,1)} %x_ref.1, bf16[4096,1792]{1,0:T(8,128)(2,1)} %wg_ref.1, bf16[4096,1792]{1,0:T(8,128)(2,1)} %wu_ref.1, bf16[1792,4096]{1,0:T(8,128)(2,1)} %wd_ref.1), custom_call_target="tpu_custom_call" | custom-call | flops 90194313216 | bytes 161480704 | tf_op jit(solution)/shard_map/mlp_ring/pallas_call | solution.py:264
  324.3 1.3 copy.6

commit v7 on v5

--- a/solution.py
+++ b/solution.py
@@ -8,7 +8,7 @@
 from jax.sharding import PartitionSpec as P
 
 MESH = pl.DeviceIdType.MESH
-VMEM_LIMIT = 61 * 2**20 + 2**19
+VMEM_LIMIT = 57 * 2**20 + 2**19
 SUBS = 2
 
 
@@ -18,6 +18,7 @@
     wg_ref,
     wu_ref,
     wd_ref,
+    acc,
     y_ref,
     xg_ref,
     rs_ref,
@@ -27,7 +28,6 @@
     hid,
     xbuf,
     sbuf,
-    acc,
     ag_send,
     ag_recv,
     rs_send,
@@ -245,12 +245,6 @@
     for s in range(SUBS):
         for d in range(2):
             reduce(0, s, d, s, last=True).wait_recv()
-        for d in range(2):
-            o = home(0, s, d)
-            y_ref[o, :] = (acc[o, :] + y_ref[o, :].astype(jnp.float32)).astype(jnp.bfloat16)
-
-    for s in range(SUBS):
-        for d in range(2):
             reduce(0, s, d, s, last=True).wait_send()
 
 
@@ -264,16 +258,18 @@
         piece = rows // (2 * SUBS)
         flops = 6 * n * rows * dim * hidden
         wire = 2 * batches * rows * dim * 2
+        vmem_space = pl.BlockSpec(memory_space=pltpu.MemorySpace.VMEM)
         any_space = pl.BlockSpec(memory_space=pltpu.MemorySpace.HBM)
-        y, _, _ = pl.pallas_call(
+        total, last, _, _ = pl.pallas_call(
             functools.partial(_kernel, n),
             out_shape=(
+                pltpu.VMEM((rows, dim), jnp.float32),
                 pltpu.VMEM((rows, dim), jnp.bfloat16),
                 jax.ShapeDtypeStruct((batches, rows, dim), jnp.bfloat16),
                 jax.ShapeDtypeStruct((batches - 1, rows, dim), jnp.bfloat16),
             ),
             in_specs=[any_space] * 4,
-            out_specs=(pl.BlockSpec(memory_space=pltpu.MemorySpace.VMEM), any_space, any_space),
+            out_specs=(vmem_space, vmem_space, any_space, any_space),
             scratch_shapes=[
                 pltpu.VMEM(w_gate.shape, jnp.bfloat16),
                 pltpu.VMEM(w_up.shape, jnp.bfloat16),
@@ -281,7 +277,6 @@
                 pltpu.VMEM((batches, rows, hidden), jnp.bfloat16),
                 pltpu.VMEM((2, rows, dim), jnp.bfloat16),
                 pltpu.VMEM((2 * SUBS, 2 * piece, dim), jnp.bfloat16),
-                pltpu.VMEM((rows, dim), jnp.float32),
                 pltpu.SemaphoreType.DMA((batches, SUBS, 2)),
                 pltpu.SemaphoreType.DMA((batches, SUBS, 2)),
                 pltpu.SemaphoreType.DMA((batches, SUBS, 2)),
@@ -299,7 +294,7 @@
             ),
             name="mlp_ring",
         )(x, w_gate, w_up, w_down)
-        return y
+        return (total + last.astype(jnp.float32)).astype(jnp.bfloat16)
 
     return jax.shard_map(
         step,

time: 326 us -> 326 us (level)
  no operation moved by 1% of the time
where the time goes in v7:
time: 326 us
  Pallas kernels  324 us (99%)
    pallas_call x1, Pallas kernels, step(): pl.pallas_call(functools.partial(_kernel, n), out_shape=(pltpu.VMEM((rows...  324 us

profile of v7, /device:TPU:21, one launch (start us, length us, event | category | flops | bytes accessed | tf_op | source)
XLA Modules:
  0.0 326.0 jit_solution(6044259752217651933)
XLA Ops:
  0.0 324.1 %mlp_ring.1 = (f32[256,4096]{1,0:T(8,128)S(1)}, bf16[256,4096]{1,0:T(8,128)(2,1)S(1)}, bf16[7,256,4096]{2,1,0:T(8,128)(2,1)}, bf16[6,256,4096]{2,1,0:T(8,128)(2,1)}) custom-call(bf16[256,4096]{1,0:T(8,128)(2,1)} %x_ref.1, bf16[4096,1792]{1,0:T(8,128)(2,1)} %wg_ref.1, bf16[4096,1792]{1,0:T(8,128)(2,1)} %wu_ref.1, bf16[1792,4096]{1,0:T(8,128)(2,1)} %wd_ref.1), custom_call_target="tpu_custom_call" | custom-call | flops 90194313216 | bytes 161480704 | tf_op jit(solution)/shard_map/mlp_ring/pallas_call | solution.py:263
  324.1 1.9 add_convert_fusion
